TPU v7x, 128 devices: a whole 4x4x4 slice. The times are simulated.
128 devices in a mesh: att: 4 (over x), emb: 32 (over z, y, core).
Axes of the slice: x: 4, y: 4, z: 4, core: 2. Of those that a mesh axis runs over, the one named last changes fastest.
Arguments:
- w_qkv: float32 [4, 3, 2560, 2048], P(None, None, 'emb', 'att')
- w_out: float32 [4, 2048, 2560], P(None, 'att', 'emb')
- x_in: bfloat16 [4, 6144, 2560], P(None, None, 'emb')
- dy_qkv: bfloat16 [4, 3, 6144, 2048], P(None, None, None, 'att')
- x_attn: bfloat16 [4, 6144, 2048], P(None, None, 'att')
- dy_out: bfloat16 [4, 6144, 2560], P(None, None, 'emb')
- r_qkv: float32 [4, 3, 2560], P(None, None, 'emb')
- c_qkv: float32 [4, 3, 2048], P(None, None, 'att')
- r_out: float32 [4, 2048], P(None, 'att')
- c_out: float32 [4, 2560], P(None, 'emb')
- hyper_params: float32 [3], replicated
Outputs:
- output 1: float32 [4, 3, 2560, 2048], P(None, None, 'emb', 'att')
- output 2: float32 [4, 2048, 2560], P(None, 'att', 'emb')
- output 3: float32 [4, 3, 2560], P(None, None, 'emb')
- output 4: float32 [4, 3, 2048], P(None, None, 'att')
- output 5: float32 [4, 2048], P(None, 'att')
- output 6: float32 [4, 2560], P(None, 'emb')
All inputs are finite; a program needn't handle non-finite values.
Results may differ from a plain program's by a relative error of at most 0.001.
Values are sent between devices in bfloat16 or wider.
A program may use at most 1 GiB of HBM per device.

v0:
```python
import jax
import jax.numpy as jnp
from jax import lax
from jax.sharding import PartitionSpec as P

EPS_SQUARE = 1e-30
EPS_SCALE = 1e-3


def factored_step(w_grad, weight, row_old, col_old, hyper_params, m_axis, n_axis, m_total, n_total):
    beta_two = hyper_params[0]
    rel_step = hyper_params[1]
    clip_limit = hyper_params[2]
    q_sq = w_grad * w_grad + EPS_SQUARE
    row_part = jnp.sum(q_sq, axis=2)
    col_part = jnp.sum(q_sq, axis=1)
    lead_flag = (lax.axis_index(n_axis) == 0).astype(jnp.float32)
    scalar_part = jnp.stack(
        [jnp.sum(col_part, axis=1), jnp.sum(weight * weight, axis=(1, 2)), lead_flag * jnp.sum(row_old, axis=1)],
        axis=1,
    )
    row_sum = lax.psum(row_part, n_axis)
    col_sum = lax.psum(col_part, m_axis)
    scalar_sum = lax.psum(scalar_part, (m_axis, n_axis))
    n_elems = m_total * n_total
    row_new = beta_two * row_old + (1.0 - beta_two) * (row_sum / n_total)
    col_new = beta_two * col_old + (1.0 - beta_two) * (col_sum / m_total)
    mean_row = beta_two * scalar_sum[:, 2] / m_total + (1.0 - beta_two) * scalar_sum[:, 0] / n_elems
    row_factor = lax.rsqrt(row_new / mean_row[:, None])
    col_factor = lax.rsqrt(col_new)
    update = w_grad * row_factor[:, :, None] * col_factor[:, None, :]
    u_sum = lax.psum(jnp.sum(update * update, axis=(1, 2)), (m_axis, n_axis))
    rms_u = jnp.sqrt(u_sum / n_elems)
    rms_w = jnp.sqrt(scalar_sum[:, 1] / n_elems)
    step_size = rel_step * jnp.maximum(EPS_SCALE, rms_w) / jnp.maximum(1.0, rms_u / clip_limit)
    return weight - step_size[:, None, None] * update, row_new, col_new


def solution(mesh):
    emb_size = mesh.shape["emb"]
    att_size = mesh.shape["att"]
    in_specs = (
        P(None, None, "emb", "att"),
        P(None, "att", "emb"),
        P(None, None, "emb"),
        P(None, None, None, "att"),
        P(None, None, "att"),
        P(None, None, "emb"),
        P(None, None, "emb"),
        P(None, None, "att"),
        P(None, "att"),
        P(None, "emb"),
        P(),
    )
    out_specs = (
        P(None, None, "emb", "att"),
        P(None, "att", "emb"),
        P(None, None, "emb"),
        P(None, None, "att"),
        P(None, "att"),
        P(None, "emb"),
    )

    def local_run(w_qkv, w_out, x_in, dy_qkv, x_attn, dy_out, r_qkv, c_qkv, r_out, c_out, hyper_params):
        d_model = x_in.shape[2] * emb_size
        inner_dim = x_attn.shape[2] * att_size
        per_layer = []
        for layer_idx in range(w_qkv.shape[0]):
            g_qkv = jnp.einsum("td,ktn->kdn", x_in[layer_idx], dy_qkv[layer_idx], preferred_element_type=jnp.float32)
            new_qkv = factored_step(
                g_qkv, w_qkv[layer_idx], r_qkv[layer_idx], c_qkv[layer_idx], hyper_params, "emb", "att", d_model, inner_dim
            )
            g_out = jnp.einsum("ti,td->id", x_attn[layer_idx], dy_out[layer_idx], preferred_element_type=jnp.float32)
            new_out = factored_step(
                g_out[None], w_out[layer_idx][None], r_out[layer_idx][None], c_out[layer_idx][None],
                hyper_params, "att", "emb", inner_dim, d_model
            )
            per_layer.append((new_qkv[0], new_out[0][0], new_qkv[1], new_qkv[2], new_out[1][0], new_out[2][0]))
        return tuple(jnp.stack([layer_out[out_slot] for layer_out in per_layer]) for out_slot in range(6))

    return jax.shard_map(local_run, mesh=mesh, in_specs=in_specs, out_specs=out_specs, check_vma=False)
```

profile of v0, /device:TPU:1, one launch (start us, length us, event | category | flops | bytes accessed | tf_op | source)
XLA Modules:
  0.0 539.0 jit_solution(5850868492575967866)
XLA Ops:
  6.8 1.9 fusion.47
  8.7 1.9 multiply_reduce_fusion.11
  13.0 5.0 fusion.64
  19.3 4.7 fusion.61
  25.4 5.3 fusion.70
  32.0 5.4 fusion.67
  38.8 68.6 %all-reduce.1 = (f32[1,3]{1,0:T(1,128)S(1)}, f32[1,3]{1,0:T(1,128)S(1)}, f32[1,3]{1,0:T(1,128)S(1)}, f32[1,3]{1,0:T(1,128)S(1)}) all-reduce(f32[1,3]{1,0:T(1,128)S(1)} %pad_maximum_fusion.13, f32[1,3]{1,0:T(1,128)S(1)} %pad_maximum_fusion.12, f32[1,3]{1,0:T(1,128)S(1)} %pad_maximum_fusion.11, ...), channel_id=1, replica_groups=mesh['att'=4,'emb'=32] {'att','emb'}, use_global_device_ids=true, to_apply=%region_73.0 | all-reduce | flops 12 | bytes 96 | tf_op jit(solution)/shard_map/psum | solution.py:24
  121.8 10.9 %fusion.52 = (f32[3,80]{1,0:T(4,128)S(1)}, f32[3,512]{1,0:T(4,128)S(1)}, f32[3]{0:T(128)S(1)}, f32[3,512,80]{1,2,0:T(8,128)}) fusion(bf16[4,3,6144,512]{3,2,1,0:T(8,128)(2,1)} %param.14, bf16[4,6144,80]{1,2,0:T(8,128)(2,1)} %param.13), kind=kOutput, calls=%fused_computation.74 | convolution fusion | flops 1510562048 | bytes 20356044 | tf_op jit(solution)/shard_map/td,ktn->kdn/dot_general | solution.py:69
  132.8 9.7 %fusion.49 = (f32[3,80]{1,0:T(4,128)}, f32[3,512]{1,0:T(4,128)S(1)}, f32[3]{0:T(128)S(1)}, f32[3,512,80]{1,2,0:T(8,128)}) fusion(bf16[4,3,6144,512]{3,2,1,0:T(8,128)(2,1)} %param.14, bf16[4,6144,80]{1,2,0:T(8,128)(2,1)S(1)} %copy-done.9), kind=kOutput, calls=%fused_computation.71 | convolution fusion | flops 1510562048 | bytes 20356044 | tf_op jit(solution)/shard_map/td,ktn->kdn/dot_general | solution.py:69
  142.5 9.7 %fusion.58 = (f32[3,80]{1,0:T(4,128)}, f32[3,512]{1,0:T(4,128)S(1)}, f32[3]{0:T(128)S(1)}, f32[3,512,80]{1,2,0:T(8,128)}) fusion(bf16[4,3,6144,512]{3,2,1,0:T(8,128)(2,1)} %param.14, bf16[4,6144,80]{1,2,0:T(8,128)(2,1)S(1)} %copy-done.9), kind=kOutput, calls=%fused_computation.80 | convolution fusion | flops 1510562048 | bytes 20356044 | tf_op jit(solution)/shard_map/td,ktn->kdn/dot_general | solution.py:69
  152.3 9.0 %fusion.55 = (f32[3,80]{1,0:T(4,128)}, f32[3,512]{1,0:T(4,128)S(1)}, f32[3]{0:T(128)}, f32[3,512,80]{1,2,0:T(8,128)S(1)}) fusion(bf16[4,3,6144,512]{3,2,1,0:T(8,128)(2,1)} %param.14, bf16[4,6144,80]{1,2,0:T(8,128)(2,1)S(1)} %copy-done.9), kind=kOutput, calls=%fused_computation.77 | convolution fusion | flops 1510562048 | bytes 20356044 | tf_op jit(solution)/shard_map/td,ktn->kdn/dot_general | solution.py:69
  161.2 12.7 %all-reduce.5 = (f32[3,80]{1,0:T(4,128)}, f32[3,80]{1,0:T(4,128)}, f32[3,80]{1,0:T(4,128)}, f32[3,80]{1,0:T(4,128)}, f32[1,80]{1,0:T(1,128)}, /*index=5*/f32[1,80]{1,0:T(1,128)}, f32[1,80]{1,0:T(1,128)}, f32[1,80]{1,0:T(1,128)}) all-reduce(f32[3,80]{1,0:T(4,128)} %get-tuple-element.29, ...), channel_id=1, replica_groups=mesh['att'=4,'emb'=32] {'att'}, use_global_device_ids=true, to_apply=%region_35.0 | all-reduce | flops 1280 | bytes 10240 | tf_op jit(solution)/shard_map/psum | solution.py:22
  174.6 66.1 %all-reduce.3 = (f32[3,3]{0,1:T(4,128)S(1)}, f32[3,3]{0,1:T(4,128)S(1)}, f32[3,3]{0,1:T(4,128)}, f32[3,3]{0,1:T(4,128)}) all-reduce(f32[3,3]{0,1:T(4,128)S(1)} %pad_maximum_fusion.8, f32[3,3]{0,1:T(4,128)S(1)} %pad_maximum_fusion.7, f32[3,3]{0,1:T(4,128)S(1)} %pad_maximum_fusion.6, ...), channel_id=1, replica_groups=mesh['att'=4,'emb'=32] {'emb','att'}, use_global_device_ids=true, to_apply=%region_33.0 | all-reduce | flops 36 | bytes 288 | tf_op jit(solution)/shard_map/psum | solution.py:24
  248.9 2.1 rsqrt_bitcast_fusion.3
  251.5 120.8 %all-reduce.4 = (f32[3,512]{1,0:T(4,128)}, f32[3,512]{1,0:T(4,128)S(1)}, f32[3,512]{1,0:T(4,128)S(1)}, f32[3,512]{1,0:T(4,128)S(1)}, f32[1,512]{1,0:T(1,128)}, /...) all-reduce(f32[3,512]{1,0:T(4,128)S(1)} %get-tuple-element.30, ...), channel_id=1, replica_groups=mesh['att'=4,'emb'=32] {'emb'}, use_global_device_ids=true, to_apply=%region_37.0 | all-reduce | flops 8192 | bytes 65536 | tf_op jit(solution)/shard_map/psum | solution.py:23
  373.6 1.9 multiply_reduce_fusion
  377.0 1.9 divide_rsqrt_fusion.3
  380.5 1.7 multiply_reduce_fusion.6
  385.0 67.6 %all-reduce = (f32[1]{0:T(128)}, f32[1]{0:T(128)}, f32[1]{0:T(128)}, f32[1]{0:T(128)}) all-reduce(f32[1]{0:T(128)} %bitcast.117, f32[1]{0:T(128)} %bitcast.101, f32[1]{0:T(128)} %bitcast.85, f32[1]{0:T(128)} %bitcast.69), channel_id=1, replica_groups=mesh['att'=4,'emb'=32] {'att','emb'}, use_global_device_ids=true, to_apply=%region_79.0 | all-reduce | flops 4 | bytes 32 | tf_op jit(solution)/shard_map/psum | solution.py:32
  464.6 62.8 %all-reduce.2 = (f32[3]{0:T(128)S(1)}, f32[3]{0:T(128)S(1)}, f32[3]{0:T(128)S(1)}, f32[3]{0:T(128)S(1)}) all-reduce(f32[3]{0:T(128)} %multiply_reduce_fusion, f32[3]{0:T(128)} %multiply_reduce_fusion.1, f32[3]{0:T(128)S(1)} %multiply_reduce_fusion.2, f32[3]{0:T(128)S(1)} %multiply_reduce_fusion.3), channel_id=1, replica_groups=mesh['att'=4,'emb'=32] {'emb','att'}, use_global_device_ids=true, to_apply=%region_39.0 | all-reduce | flops 12 | bytes 96 | tf_op jit(solution)/shard_map/psum | solution.py:32
  527.4 1.9 bitcast_divide_fusion.3
  529.3 1.9 bitcast_divide_fusion.2
  531.2 1.9 bitcast_divide_fusion.1
  533.4 1.9 bitcast_divide_fusion
  (65 shorter events, 39.4 us)
Async XLA Ops:
  6.8 12.5 %copy-start.8 = (bf16[4,6144,80]{1,2,0:T(8,128)(2,1)S(1)}, bf16[4,6144,80]{1,2,0:T(8,128)(2,1)}, u32[]{:S(2)}) copy-start(bf16[4,6144,80]{1,2,0:T(8,128)(2,1)} %param.16) | copy-start | bytes 11796484
  121.8 10.9 %copy-start.9 = (bf16[4,6144,80]{1,2,0:T(8,128)(2,1)S(1)}, bf16[4,6144,80]{1,2,0:T(8,128)(2,1)}, u32[]{:S(2)}) copy-start(bf16[4,6144,80]{1,2,0:T(8,128)(2,1)} %param.13) | copy-start | bytes 11796484
  152.2 9.0 %copy-start.5 = (f32[3,80]{1,0:T(4,128)S(1)}, f32[3,80]{1,0:T(4,128)}, u32[]{:S(2)}) copy-start(f32[3,80]{1,0:T(4,128)} %get-tuple-element.20) | copy-start | bytes 2884
  152.2 224.8 %copy-start.2 = (f32[4,512]{1,0:T(4,128)S(1)}, f32[4,512]{1,0:T(4,128)}, u32[]{:S(2)}) copy-start(f32[4,512]{1,0:T(4,128)} %param.19) | copy-start | bytes 24580
  152.2 305.6 %copy-start.1 = (f32[4,512,80]{1,2,0:T(8,128)S(1)}, f32[4,512,80]{1,2,0:T(8,128)}, u32[]{:S(2)}) copy-start(f32[4,512,80]{1,2,0:T(8,128)} %param.12) | copy-start | bytes 1966084
  161.2 372.0 %copy-start = (f32[4,3,80,512]{3,2,1,0:T(8,128)S(1)}, f32[4,3,80,512]{3,2,1,0:T(8,128)}, u32[]{:S(2)}) copy-start(f32[4,3,80,512]{3,2,1,0:T(8,128)} %param.11) | copy-start | bytes 5898244
  240.6 10.3 %copy-start.6 = (f32[3,3]{0,1:T(4,128)}, f32[3,3]{0,1:T(4,128)S(1)}, u32[]{:S(2)}) copy-start(f32[3,3]{0,1:T(4,128)S(1)} %get-tuple-element.64) | copy-start | bytes 112
  240.6 10.3 %copy-start.7 = (f32[3,3]{0,1:T(4,128)}, f32[3,3]{0,1:T(4,128)S(1)}, u32[]{:S(2)}) copy-start(f32[3,3]{0,1:T(4,128)S(1)} %get-tuple-element.65) | copy-start | bytes 112
  459.9 78.5 %copy-start.3 = (f32[1,512]{1,0:T(1,128)S(1)}, f32[1,512]{1,0:T(1,128)}, u32[]{:S(2)}) copy-start(f32[1,512]{1,0:T(1,128)} %get-tuple-element.121) | copy-start | bytes 6148
  459.9 78.5 %copy-start.4 = (f32[1,512]{1,0:T(1,128)S(1)}, f32[1,512]{1,0:T(1,128)}, u32[]{:S(2)}) copy-start(f32[1,512]{1,0:T(1,128)} %get-tuple-element.123) | copy-start | bytes 6148
where the time goes:
time: 541 us; the launch traced here: 539 us
  blocking collectives  398 us (74%)
  matrix products  59.6 us (11%)
  other arithmetic  53.6 us (10%)
  between operations  22.5 us (4%)
    psum x2, blocking collectives, factored_step(): scalar_sum = lax.psum(scalar_part, (m_axis, n_axis))  135 us
    psum x2, blocking collectives, factored_step(): u_sum = lax.psum(jnp.sum(update * update, axis=(1, 2)), (m_axis, n_axis))  130 us
    psum x1, blocking collectives, factored_step(): col_sum = lax.psum(col_part, m_axis)  121 us
    dot_general x4, matrix products, local_run(): jnp.einsum('td,ktn->kdn', x_in[layer_idx], dy_qkv[layer_idx], preferred_e...  39.3 us
    dot_general x4, matrix products, local_run(): jnp.einsum('ti,td->id', x_attn[layer_idx], dy_out[layer_idx], preferred_e...  20.3 us
    another operation x15, other arithmetic, local_run(): jnp.stack([layer_out[out_slot] for layer_out in per_layer])  13.5 us
    psum x1, blocking collectives, factored_step(): row_sum = lax.psum(row_part, n_axis)  12.7 us
    reduce_sum x8, other arithmetic, factored_step(): u_sum = lax.psum(jnp.sum(update * update, axis=(1, 2)), (m_axis, n_axis))  11.3 us

commit v1 on v0

v1 whole, which is shorter than its diff:
```python
import functools
import jax
import jax.numpy as jnp
from jax import lax
from jax.experimental import pallas as pl
from jax.experimental.pallas import tpu as pltpu
from jax.sharding import PartitionSpec as P

EPS_SQUARE = 1e-30
EPS_SCALE = 1e-3
LANES = 128
MATS = 4
SLOTS = 3
PIECES = 4
MESH = pl.DeviceIdType.MESH


def adafactor_kernel(
    n_att, n_emb,
    xt, dt, dyq, xa, wq, wo, rq, cq, ro, co, hyp,
    wq_new, wo_new, rq_new, cq_new, ro_new, co_new,
    bbuf, abuf, g, wqv, wov, rqv, cqv, rov, cov, hv, qrecv, precv, urecv,
    bsem, asem, wsem, ssem, qsend_sem, qrecv_sem, psend_sem, precv_sem, usend_sem, urecv_sem,
):
    layers, p_loc, tokens = xt.shape
    q_loc = dyq.shape[3]
    n_mats = layers * MATS
    n_dev = n_att * n_emb
    d_model, inner = p_loc * n_emb, q_loc * n_att
    rows = tokens // PIECES
    q_rows = q_loc // LANES
    me_a, me_e = lax.axis_index("att"), lax.axis_index("emb")
    me = me_a * n_emb + me_e

    def device_of(flat):
        return {"att": flat // n_emb, "emb": lax.rem(flat, n_emb)}

    barrier = pltpu.get_barrier_semaphore()

    def greet(j, carry):
        pl.semaphore_signal(barrier, inc=1, device_id=device_of(lax.rem(me + j, n_dev)), device_id_type=MESH)
        return carry

    lax.fori_loop(1, n_dev, greet, 0)

    def start_a(src, layer, slot):
        pltpu.make_async_copy(src.at[layer], abuf.at[slot], asem.at[slot]).start()

    def start_b(mat, slot):
        layer, kind = mat // MATS, lax.rem(mat, MATS)

        def pieces(src):
            for k in range(PIECES):
                part = pl.ds(k * rows, rows)
                pltpu.make_async_copy(src.at[part], bbuf.at[slot, part], bsem.at[slot, k]).start()

        @pl.when(kind < MATS - 1)
        def _():
            pieces(dyq.at[layer, kind])

        @pl.when(kind == MATS - 1)
        def _():
            pieces(xa.at[layer])

    start_a(xt, 0, 0)
    for mat in range(SLOTS):
        for k in range(PIECES):
            part = pl.ds(k * rows, rows)
            pltpu.make_async_copy(dyq.at[0, mat, part], bbuf.at[mat, part], bsem.at[mat, k]).start()
    start_a(dt, 0, 1)
    small = [
        pltpu.make_async_copy(src, dst, ssem.at[k])
        for k, (src, dst) in enumerate([(rq, rqv), (cq, cqv), (ro, rov), (co, cov), (hyp, hv)])
    ]
    w_copies = [pltpu.make_async_copy(wq, wqv, wsem.at[0]), pltpu.make_async_copy(wo, wov, wsem.at[1])]
    for copy in small + w_copies:
        copy.start()

    def stream(mat, carry):
        slot = lax.rem(mat, SLOTS)
        layer, kind = mat // MATS, lax.rem(mat, MATS)
        a_slot = 2 * layer + kind // (MATS - 1)

        @pl.when(lax.rem(kind, MATS - 1) == 0)
        def _():
            pltpu.make_async_copy(xt.at[0], abuf.at[a_slot], asem.at[a_slot]).wait()

        @pl.when((kind == 0) & (layer < layers - 1))
        def _():
            start_a(xt, layer + 1, 2 * layer + 2)
            start_a(dt, layer + 1, 2 * layer + 3)

        acc = jnp.zeros((p_loc, q_loc), jnp.float32)
        for k in range(PIECES):
            part = pl.ds(k * rows, rows)
            pltpu.make_async_copy(dyq.at[0, 0, part], bbuf.at[slot, part], bsem.at[slot, k]).wait()
            acc += jnp.dot(abuf[a_slot, :, part], bbuf[slot, part, :], preferred_element_type=jnp.float32)
        g[mat] = acc

        @pl.when(mat + SLOTS < n_mats)
        def _():
            start_b(mat + SLOTS, slot)

        q_sq = acc * acc + EPS_SQUARE
        q_part = jnp.sum(q_sq, axis=0, keepdims=True)
        folded = q_sq[:, :LANES]
        for k in range(1, q_rows):
            folded += q_sq[:, k * LANES:(k + 1) * LANES]
        padded = jnp.concatenate([folded, jnp.zeros((LANES - p_loc, LANES), jnp.float32)], axis=0)
        for k in range(q_rows):
            qrecv[me_e, mat, k:k + 1, :] = q_part[:, k * LANES:(k + 1) * LANES]
        precv[me_a, mat] = jnp.sum(padded.T, axis=0, keepdims=True)
        return carry

    def q_copy(lo, hi, event, peer):
        span = qrecv.at[me_e, pl.ds(lo, hi - lo)]
        return pltpu.make_async_remote_copy(
            src_ref=span, dst_ref=span, send_sem=qsend_sem.at[event], recv_sem=qrecv_sem.at[event],
            device_id={"att": me_a, "emb": peer}, device_id_type=MESH)

    def p_copy(lo, hi, event, peer):
        span = precv.at[me_a, pl.ds(lo, hi - lo)]
        return pltpu.make_async_remote_copy(
            src_ref=span, dst_ref=span, send_sem=psend_sem.at[event], recv_sem=precv_sem.at[event],
            device_id={"att": peer, "emb": me_e}, device_id_type=MESH)

    def u_copy(flat):
        return pltpu.make_async_remote_copy(
            src_ref=urecv.at[me], dst_ref=urecv.at[me], send_sem=usend_sem, recv_sem=urecv_sem,
            device_id=device_of(flat), device_id_type=MESH)

    def send(lo, hi, event):
        def to_emb(j, carry):
            q_copy(lo, hi, event, lax.rem(me_e + j, n_emb)).start()
            return carry

        def to_att(j, carry):
            p_copy(lo, hi, event, lax.rem(me_a + j, n_att)).start()
            return carry

        lax.fori_loop(1, n_emb, to_emb, 0)
        lax.fori_loop(1, n_att, to_att, 0)

    def wait_bytes(ref, sem):
        pltpu.make_async_copy(ref, ref, sem).wait()

    lane = lax.broadcasted_iota(jnp.int32, (1, LANES), 1)

    def process(lo, hi, event, u_row):
        wait_bytes(qrecv.at[pl.ds(0, n_emb - 1), pl.ds(lo, hi - lo)], qrecv_sem.at[event])
        wait_bytes(precv.at[pl.ds(0, n_att - 1), pl.ds(lo, hi - lo)], precv_sem.at[event])
        beta = hv[0:1, 0:1]
        for mat in range(lo, hi):
            layer, kind = mat // MATS, mat % MATS
            is_out = kind == MATS - 1
            q_sum = qrecv[0, mat]
            for peer in range(1, n_emb):
                q_sum += qrecv[peer, mat]
            p_sum = precv[0, mat]
            for peer in range(1, n_att):
                p_sum += precv[peer, mat]
            q_add = (1.0 - beta) * (q_sum / d_model)
            p_new_all = (1.0 - beta) * (p_sum / inner)
            p_old = cov[layer:layer + 1, :] if is_out else rqv[kind, layer:layer + 1, :]
            p_new = beta * p_old + p_new_all[:, :p_loc]
            q_parts = []
            for k in range(q_rows):
                cols = slice(k * LANES, (k + 1) * LANES)
                q_old = rov[layer:layer + 1, cols] if is_out else cqv[kind, layer:layer + 1, cols]
                q_new = beta * q_old + q_add[k:k + 1, :]
                if is_out:
                    ro_new[layer:layer + 1, cols] = q_new
                else:
                    cq_new[kind, layer:layer + 1, cols] = q_new
                q_parts.append(q_new)
            if is_out:
                co_new[layer:layer + 1, :] = p_new
                r_total = jnp.sum(sum(q_parts[1:], q_parts[0]), axis=1, keepdims=True)
            else:
                rq_new[kind, layer:layer + 1, :] = p_new
                r_total = jnp.sum(p_new, axis=1, keepdims=True)
            p_fac = jnp.concatenate([lax.rsqrt(p_new), jnp.zeros((1, LANES - p_loc), jnp.float32)], axis=1)
            p_fac = jnp.broadcast_to(p_fac, (LANES, LANES)).T[:p_loc, :]
            u_sum = jnp.zeros((p_loc, LANES), jnp.float32)
            w_sum = jnp.zeros((p_loc, LANES), jnp.float32)
            for k in range(q_rows):
                cols = slice(k * LANES, (k + 1) * LANES)
                upd = (g[mat, :, cols] * p_fac) * lax.rsqrt(q_parts[k])
                g[mat, :, cols] = upd
                w = wov[layer, :, cols] if is_out else wqv[layer, kind, :, cols]
                u_sum += upd * upd
                w_sum += w * w
            u_total = jnp.sum(jnp.sum(u_sum, axis=0, keepdims=True), axis=1, keepdims=True)
            w_total = jnp.sum(jnp.sum(w_sum, axis=0, keepdims=True), axis=1, keepdims=True)
            copies = n_emb if is_out else n_att
            mean_row = r_total / (copies * (inner if is_out else d_model))
            u_row = jnp.where(lane == mat, u_total, u_row)
            u_row = jnp.where(lane == n_mats + mat, w_total, u_row)
            u_row = jnp.where(lane == 2 * n_mats + mat, mean_row, u_row)
        return u_row

    groups = [(MATS * layer, MATS * (layer + 1)) for layer in range(layers - 1)]
    groups += [(n_mats - MATS, n_mats - 1), (n_mats - 1, n_mats)]
    u_row = jnp.zeros((1, LANES), jnp.float32)
    for event, (lo, hi) in enumerate(groups):
        lax.fori_loop(lo, hi, stream, 0)
        if event == 0:
            pl.semaphore_wait(barrier, n_dev - 1)
        send(lo, hi, event)
        if event == 0:
            for copy in small + w_copies:
                copy.wait()
        else:
            u_row = process(*groups[event - 1], event - 1, u_row)
    u_row = process(*groups[-1], len(groups) - 1, u_row)

    urecv[me] = u_row

    def to_all(j, carry):
        u_copy(lax.rem(me + j, n_dev)).start()
        return carry

    lax.fori_loop(1, n_dev, to_all, 0)
    wait_bytes(urecv.at[pl.ds(0, n_dev - 1)], urecv_sem)
    total = urecv[0]
    for peer in range(1, n_dev):
        total += urecv[peer]
    w_total = pltpu.roll(total, LANES - n_mats, 1)
    mean_row = pltpu.roll(total, LANES - 2 * n_mats, 1)
    n_elems = d_model * inner
    rel_step, clip_limit = hv[0:1, 1:2], hv[0:1, 2:3]
    rms_u = jnp.sqrt(mean_row * total / n_elems)
    rms_w = jnp.sqrt(w_total / n_elems)
    scale = rel_step * jnp.maximum(EPS_SCALE, rms_w) / jnp.maximum(1.0, rms_u / clip_limit) * jnp.sqrt(mean_row)
    for mat in range(n_mats):
        layer, kind = mat // MATS, mat % MATS
        factor = scale[:, mat:mat + 1]
        if kind == MATS - 1:
            wo_new[layer] = wov[layer] - factor * g[mat]
        else:
            wq_new[layer, kind] = wqv[layer, kind] - factor * g[mat]

    for event, (lo, hi) in enumerate(groups):
        wait_bytes(qrecv.at[pl.ds(0, n_emb - 1), pl.ds(lo, hi - lo)], qsend_sem.at[event])
        wait_bytes(precv.at[pl.ds(0, n_att - 1), pl.ds(lo, hi - lo)], psend_sem.at[event])
    wait_bytes(urecv.at[pl.ds(0, n_dev - 1)], usend_sem)


def solution(mesh):
    n_emb = mesh.shape["emb"]
    n_att = mesh.shape["att"]
    in_specs = (
        P(None, None, "emb", "att"),
        P(None, "att", "emb"),
        P(None, None, "emb"),
        P(None, None, None, "att"),
        P(None, None, "att"),
        P(None, None, "emb"),
        P(None, None, "emb"),
        P(None, None, "att"),
        P(None, "att"),
        P(None, "emb"),
        P(),
    )
    out_specs = (
        P(None, None, "emb", "att"),
        P(None, "att", "emb"),
        P(None, None, "emb"),
        P(None, None, "att"),
        P(None, "att"),
        P(None, "emb"),
    )

    def local_run(w_qkv, w_out, x_in, dy_qkv, x_attn, dy_out, r_qkv, c_qkv, r_out, c_out, hyper_params):
        f32, bf16 = jnp.float32, jnp.bfloat16
        layers, tokens, p_loc = x_in.shape
        q_loc = x_attn.shape[2]
        n_mats, n_groups = layers * MATS, layers + 1
        args = (
            jnp.swapaxes(x_in, 1, 2), jnp.swapaxes(dy_out, 1, 2), dy_qkv, x_attn,
            w_qkv, jnp.swapaxes(w_out, 1, 2),
            jnp.swapaxes(r_qkv, 0, 1), jnp.swapaxes(c_qkv, 0, 1), r_out, c_out, hyper_params.reshape(1, 3),
        )
        sds = jax.ShapeDtypeStruct
        wo_shape = (layers, p_loc, q_loc)
        rq_shape, cq_shape = (3, layers, p_loc), (3, layers, q_loc)
        out_shape = (
            sds(w_qkv.shape, f32), sds(wo_shape, f32), sds(rq_shape, f32), sds(cq_shape, f32),
            sds(r_out.shape, f32), sds(c_out.shape, f32),
        )
        dma = pltpu.SemaphoreType.DMA
        outs = pl.pallas_call(
            functools.partial(adafactor_kernel, n_att, n_emb),
            out_shape=out_shape,
            in_specs=[pl.BlockSpec(memory_space=pltpu.HBM)] * len(args),
            out_specs=[pl.BlockSpec(memory_space=pltpu.VMEM)] * len(out_shape),
            scratch_shapes=[
                pltpu.VMEM((SLOTS, tokens, q_loc), bf16),
                pltpu.VMEM((2 * layers, p_loc, tokens), bf16),
                pltpu.VMEM((n_mats, p_loc, q_loc), f32),
                pltpu.VMEM(w_qkv.shape, f32),
                pltpu.VMEM(wo_shape, f32),
                pltpu.VMEM(rq_shape, f32),
                pltpu.VMEM(cq_shape, f32),
                pltpu.VMEM(r_out.shape, f32),
                pltpu.VMEM(c_out.shape, f32),
                pltpu.VMEM((1, 3), f32),
                pltpu.VMEM((n_emb, n_mats, q_loc // LANES, LANES), f32),
                pltpu.VMEM((n_att, n_mats, 1, LANES), f32),
                pltpu.VMEM((n_att * n_emb, 1, LANES), f32),
                dma((SLOTS, PIECES)), dma((2 * layers,)), dma((2,)), dma((5,)),
                dma((n_groups,)), dma((n_groups,)), dma((n_groups,)), dma((n_groups,)), dma(()), dma(()),
            ],
            compiler_params=pltpu.CompilerParams(
                collective_id=0, has_side_effects=True, vmem_limit_bytes=48 * 1024 * 1024),
            name="adafactor",
        )(*args)
        return (
            outs[0], jnp.swapaxes(outs[1], 1, 2), jnp.swapaxes(outs[2], 0, 1), jnp.swapaxes(outs[3], 0, 1),
            outs[4], outs[5],
        )

    return jax.shard_map(local_run, mesh=mesh, in_specs=in_specs, out_specs=out_specs, check_vma=False)
```

time: 541 us -> 67 us (0.12)
  blocking collectives: 398 us -> 0 us
  matrix products: 59.6 us -> 0 us
  Pallas kernels: 0 us -> 55.4 us
  other arithmetic: 53.6 us -> 0 us
  between operations: 22.5 us -> 0.66 us
  local copies, waits for them, and re-layouts: 4.86 us -> 10.6 us
    psum x6 -> x0, blocking collectives: 398 us -> none  [the longest x2 135 us: factored_step(): scalar_sum = lax.psum(scalar_part, (m_axis, n_axis))]
    dot_general x8 -> x0, matrix products: 59.6 us -> none  [the longest x4 39.3 us: local_run(): jnp.einsum('td,ktn->kdn', x_in[layer_idx], dy_qkv[layer_idx], preferred_e...]
    pallas_call x0 -> x1, Pallas kernels: none -> 55.4 us  [local_run(): pl.pallas_call(functools.partial(adafactor_kernel, n_att, n_emb), out_sha...]
    another operation x23 -> x0, other arithmetic: 19.7 us -> none  [the longest x15 13.5 us: local_run(): jnp.stack([layer_out[out_slot] for layer_out in per_layer])]
    reduce_sum x12 -> x0, other arithmetic: 17.5 us -> none  [the longest x8 11.3 us: factored_step(): u_sum = lax.psum(jnp.sum(update * update, axis=(1, 2)), (m_axis, n_axis))]
    div x6 -> x0, other arithmetic: 9.8 us -> none  [the longest x4 7.74 us: factored_step(): rel_step * jnp.maximum(EPS_SCALE, rms_w)]
    unnamed x22 -> x20, local copies, waits for them, and re-layouts: 1.27 us -> 10.6 us
where the time goes in v1:
time: 67 us; the launch traced here: 66.6 us
  Pallas kernels  55.4 us (83%)
  local copies, waits for them, and re-layouts  10.6 us (16%)
    pallas_call x1, Pallas kernels, local_run(): pl.pallas_call(functools.partial(adafactor_kernel, n_att, n_emb), out_sha...  55.4 us
    unnamed x20, local copies, waits for them, and re-layouts  10.6 us

profile of v1, /device:TPU:1, one launch (start us, length us, event | category | flops | bytes accessed | tf_op | source)
XLA Modules:
  0.0 66.6 jit_solution(4313391391551252924)
XLA Ops:
  0.6 0.0 copy-start
  0.6 1.5 %copy-done = f32[4,3,80,512]{3,2,1,0:T(8,128)S(1)} copy-done((f32[4,3,80,512]{3,2,1,0:T(8,128)S(1)}, f32[4,3,80,512]{3,2,1,0:T(8,128)}, u32[]{:S(2)}) %copy-start) | copy-done | bytes 1966104
  2.2 0.0 copy-start.1
  2.2 1.1 %copy-done.1 = f32[4,512,80]{1,2,0:T(8,128)S(1)} copy-done((f32[4,512,80]{1,2,0:T(8,128)S(1)}, f32[4,512,80]{1,2,0:T(8,128)}, u32[]{:S(2)}) %copy-start.1) | copy-done | bytes 655384
  3.3 0.0 copy-start.2
  3.3 0.7 %copy-done.2 = f32[4,3,512]{2,0,1:T(4,128)S(1)} copy-done((f32[4,3,512]{2,0,1:T(4,128)S(1)}, f32[4,3,512]{2,0,1:T(4,128)}, u32[]{:S(2)}) %copy-start.2) | copy-done | bytes 24600
  4.0 0.0 copy-start.3
  4.0 0.7 %copy-done.3 = f32[4,512]{1,0:T(4,128)S(1)} copy-done((f32[4,512]{1,0:T(4,128)S(1)}, f32[4,512]{1,0:T(4,128)}, u32[]{:S(2)}) %copy-start.3) | copy-done | bytes 8216
  4.7 0.0 copy-start.4
  4.7 0.7 %copy-done.4 = f32[4,3,80]{2,0,1:T(4,128)S(1)} copy-done((f32[4,3,80]{2,0,1:T(4,128)S(1)}, f32[4,3,80]{2,0,1:T(4,128)}, u32[]{:S(2)}) %copy-start.4) | copy-done | bytes 3864
  5.4 0.0 copy-start.5
  5.4 0.7 %copy-done.5 = f32[4,80]{1,0:T(4,128)S(1)} copy-done((f32[4,80]{1,0:T(4,128)S(1)}, f32[4,80]{1,0:T(4,128)}, u32[]{:S(2)}) %copy-start.5) | copy-done | bytes 1304
  6.1 0.0 copy-start.6
  6.1 0.7 copy-done.6
  6.7 55.4 %adafactor.1 = (f32[4,3,80,512]{3,2,1,0:T(8,128)S(1)}, f32[4,80,512]{2,1,0:T(8,128)S(1)}, f32[3,4,80]{2,1,0:T(4,128)S(1)}, f32[3,4,512]{2,1,0:T(4,128)S(1)}, f32[4,512]{1,0:T(4,128)S(1)}, /*index=5*/f32[4,80]{1,0:T(4,128)S(1)}) custom-call(bf16[4,80,6144]{2,1,0:T(8,128)(2,1)} %bitcast.16, bf16[4,80,6144]{2,1,0:T(8,128)(2,1)} %bitcast.17, ...), custom_call_target="tpu_custom_call" | custom-call | tf_op jit(solution)/shard_map/adafactor/pallas_call | solution.py:292
  62.1 1.3 %copy.23 = f32[4,3,80,512]{3,2,1,0:T(8,128)} copy(f32[4,3,80,512]{3,2,1,0:T(8,128)S(1)} %get-tuple-element.24) | data formatting | bytes 3932160
  63.4 0.8 %copy.24 = f32[4,512,80]{1,2,0:T(8,128)} copy(f32[4,512,80]{1,2,0:T(8,128)S(1)} %bitcast.10) | data formatting | bytes 1310720
  64.3 0.6 copy.25
  64.8 0.6 copy.26
  65.5 0.6 copy.27
  66.0 0.6 copy.28
Async XLA Ops:
  0.6 1.5 %copy-start = (f32[4,3,80,512]{3,2,1,0:T(8,128)S(1)}, f32[4,3,80,512]{3,2,1,0:T(8,128)}, u32[]{:S(2)}) copy-start(f32[4,3,80,512]{3,2,1,0:T(8,128)} %wq.1) | copy-start | bytes 5898244
  2.2 1.1 %copy-start.1 = (f32[4,512,80]{1,2,0:T(8,128)S(1)}, f32[4,512,80]{1,2,0:T(8,128)}, u32[]{:S(2)}) copy-start(f32[4,512,80]{1,2,0:T(8,128)} %param.12) | copy-start | bytes 1966084
  3.3 0.7 %copy-start.2 = (f32[4,3,512]{2,0,1:T(4,128)S(1)}, f32[4,3,512]{2,0,1:T(4,128)}, u32[]{:S(2)}) copy-start(f32[4,3,512]{2,0,1:T(4,128)} %param.18) | copy-start | bytes 73732
  4.0 0.7 %copy-start.3 = (f32[4,512]{1,0:T(4,128)S(1)}, f32[4,512]{1,0:T(4,128)}, u32[]{:S(2)}) copy-start(f32[4,512]{1,0:T(4,128)} %ro.1) | copy-start | bytes 24580
  4.7 0.7 %copy-start.4 = (f32[4,3,80]{2,0,1:T(4,128)S(1)}, f32[4,3,80]{2,0,1:T(4,128)}, u32[]{:S(2)}) copy-start(f32[4,3,80]{2,0,1:T(4,128)} %param.17) | copy-start | bytes 11524
  5.4 0.7 %copy-start.5 = (f32[4,80]{1,0:T(4,128)S(1)}, f32[4,80]{1,0:T(4,128)}, u32[]{:S(2)}) copy-start(f32[4,80]{1,0:T(4,128)} %co.1) | copy-start | bytes 3844
  6.1 0.7 copy-start.6

commit v2 on v1

--- a/solution.py
+++ b/solution.py
@@ -10,64 +10,67 @@
 EPS_SCALE = 1e-3
 LANES = 128
 MATS = 4
-SLOTS = 3
-PIECES = 4
+SLOTS = 4
+PIECES = 6
+RING = 6
+LEAD = 3
 MESH = pl.DeviceIdType.MESH
 
 
 def adafactor_kernel(
     n_att, n_emb,
     xt, dt, dyq, xa, wq, wo, rq, cq, ro, co, hyp,
-    wq_new, wo_new, rq_new, cq_new, ro_new, co_new,
-    bbuf, abuf, g, wqv, wov, rqv, cqv, rov, cov, hv, qrecv, precv, urecv,
-    bsem, asem, wsem, ssem, qsend_sem, qrecv_sem, psend_sem, precv_sem, usend_sem, urecv_sem,
+    wqv, wov, g, scale_row, rq_new, cq_new, ro_new, co_new,
+    bbuf, fbuf, rbuf, abuf, rqv, cqv, rov, cov, hv, qrecv, precv, urecv,
+    bsem, fsem, fsend_sem, rsem, free_sem, asem, wsem, ssem,
+    qsend_sem, qrecv_sem, psend_sem, precv_sem, usend_sem, urecv_sem,
 ):
     layers, p_loc, tokens = xt.shape
     q_loc = dyq.shape[3]
     n_mats = layers * MATS
     n_dev = n_att * n_emb
     d_model, inner = p_loc * n_emb, q_loc * n_att
-    rows = tokens // PIECES
+    rows, main = tokens // PIECES, PIECES - 2
     q_rows = q_loc // LANES
     me_a, me_e = lax.axis_index("att"), lax.axis_index("emb")
     me = me_a * n_emb + me_e
-
-    def device_of(flat):
-        return {"att": flat // n_emb, "emb": lax.rem(flat, n_emb)}
-
-    barrier = pltpu.get_barrier_semaphore()
-
-    def greet(j, carry):
-        pl.semaphore_signal(barrier, inc=1, device_id=device_of(lax.rem(me + j, n_dev)), device_id_type=MESH)
-        return carry
-
-    lax.fori_loop(1, n_dev, greet, 0)
+    core = lax.rem(me_e, 2)
+    partner = {"att": me_a, "emb": me_e + 1 - 2 * core}
+    own_part = pl.ds(pl.multiple_of((PIECES - 1 - core) * rows, rows), rows)
+    got_part = pl.ds(pl.multiple_of((PIECES - 2 + core) * rows, rows), rows)
 
     def start_a(src, layer, slot):
         pltpu.make_async_copy(src.at[layer], abuf.at[slot], asem.at[slot]).start()
 
-    def start_b(mat, slot):
+    def start_pass(src, slot):
+        pltpu.make_async_copy(src.at[own_part], fbuf.at[slot], fsem.at[slot]).start()
+
+    def start_main(src, slot):
+        for k in range(main):
+            part = pl.ds(k * rows, rows)
+            pltpu.make_async_copy(src.at[part], bbuf.at[slot, part], bsem.at[slot, k]).start()
+
+    def of_mat(start, mat, slot):
         layer, kind = mat // MATS, lax.rem(mat, MATS)
 
-        def pieces(src):
-            for k in range(PIECES):
-                part = pl.ds(k * rows, rows)
-                pltpu.make_async_copy(src.at[part], bbuf.at[slot, part], bsem.at[slot, k]).start()
-
         @pl.when(kind < MATS - 1)
         def _():
-            pieces(dyq.at[layer, kind])
+            start(dyq.at[layer, kind], slot)
 
         @pl.when(kind == MATS - 1)
         def _():
-            pieces(xa.at[layer])
+            start(xa.at[layer], slot)
+
+    def source(mat):
+        return xa.at[mat // MATS] if mat % MATS == MATS - 1 else dyq.at[mat // MATS, mat % MATS]
 
     start_a(xt, 0, 0)
     for mat in range(SLOTS):
-        for k in range(PIECES):
-            part = pl.ds(k * rows, rows)
-            pltpu.make_async_copy(dyq.at[0, mat, part], bbuf.at[mat, part], bsem.at[mat, k]).start()
+        start_pass(source(mat), mat)
+        start_main(source(mat), mat)
     start_a(dt, 0, 1)
+    for mat in range(SLOTS, RING):
+        start_pass(source(mat), mat)
     small = [
         pltpu.make_async_copy(src, dst, ssem.at[k])
         for k, (src, dst) in enumerate([(rq, rqv), (cq, cqv), (ro, rov), (co, cov), (hyp, hv)])
@@ -76,10 +79,55 @@
     for copy in small + w_copies:
         copy.start()
 
+    side = 4
+    att_at = [lax.rem(me_a + k, n_att) for k in range(n_att)]
+    planes = n_emb // (2 * side)
+    z_at = [lax.rem(me_e // (2 * side) + k, planes) * (2 * side) for k in range(planes)]
+    y_at = [lax.rem(lax.rem(me_e, 2 * side) // 2 + k, side) * 2 for k in range(side)]
+    core_at = [core, 1 - core]
+
+    def hops(k, n):
+        return min(k, n - k)
+
+    emb_steps = sorted(
+        ((z, y, h) for z in range(planes) for y in range(side) for h in range(2) if (z, y, h) != (0, 0, 0)),
+        key=lambda s: -(hops(s[0], planes) + hops(s[1], side)))
+    emb_at = {(z, y, h): z_at[z] + y_at[y] + core_at[h] for z in range(planes) for y in range(side) for h in range(2)}
+    all_steps = sorted(
+        ((k, s) for k in range(n_att) for s in emb_at if (k, s) != (0, (0, 0, 0))),
+        key=lambda t: -(hops(t[0], n_att) + hops(t[1][0], planes) + hops(t[1][1], side)))
+
+    barrier = pltpu.get_barrier_semaphore()
+    for k, s in all_steps:
+        pl.semaphore_signal(
+            barrier, inc=1, device_id={"att": att_at[k], "emb": emb_at[s]}, device_id_type=MESH)
+    pl.semaphore_wait(barrier, n_dev - 1)
+
+    def pass_copy(slot):
+        return pltpu.make_async_remote_copy(
+            src_ref=fbuf.at[slot], dst_ref=rbuf.at[slot], send_sem=fsend_sem.at[slot], recv_sem=rsem.at[slot],
+            device_id=partner, device_id_type=MESH)
+
+    def pass_on(slot):
+        pltpu.make_async_copy(dyq.at[0, 0, pl.ds(0, rows)], fbuf.at[slot], fsem.at[slot]).wait()
+        pass_copy(slot).start()
+
+    for mat in range(LEAD):
+        pass_on(mat)
+
     def stream(mat, carry):
-        slot = lax.rem(mat, SLOTS)
+        slot, ring = lax.rem(mat, SLOTS), lax.rem(mat, RING)
         layer, kind = mat // MATS, lax.rem(mat, MATS)
         a_slot = 2 * layer + kind // (MATS - 1)
+        ahead = mat + LEAD
+
+        @pl.when(ahead < n_mats)
+        def _():
+            @pl.when(ahead >= RING)
+            def _():
+                pl.semaphore_wait(free_sem, 1)
+
+            pass_on(lax.rem(ahead, RING))
 
         @pl.when(lax.rem(kind, MATS - 1) == 0)
         def _():
@@ -90,16 +138,27 @@
             start_a(xt, layer + 1, 2 * layer + 2)
             start_a(dt, layer + 1, 2 * layer + 3)
 
-        acc = jnp.zeros((p_loc, q_loc), jnp.float32)
-        for k in range(PIECES):
+        def product(a_part, b):
+            return jnp.dot(abuf[a_slot, :, a_part], b, preferred_element_type=jnp.float32)
+
+        acc = product(own_part, fbuf[ring])
+        for k in range(main):
             part = pl.ds(k * rows, rows)
             pltpu.make_async_copy(dyq.at[0, 0, part], bbuf.at[slot, part], bsem.at[slot, k]).wait()
-            acc += jnp.dot(abuf[a_slot, :, part], bbuf[slot, part, :], preferred_element_type=jnp.float32)
+            acc += product(part, bbuf[slot, part, :])
+        pass_copy(ring).wait_recv()
+        acc += product(got_part, rbuf[ring])
         g[mat] = acc
 
+        @pl.when(mat + RING < n_mats)
+        def _():
+            pl.semaphore_signal(free_sem, inc=1, device_id=partner, device_id_type=MESH)
+            pass_copy(ring).wait_send()
+            of_mat(start_pass, mat + RING, ring)
+
         @pl.when(mat + SLOTS < n_mats)
         def _():
-            start_b(mat + SLOTS, slot)
+            of_mat(start_main, mat + SLOTS, slot)
 
         q_sq = acc * acc + EPS_SQUARE
         q_part = jnp.sum(q_sq, axis=0, keepdims=True)
@@ -124,22 +183,23 @@
             src_ref=span, dst_ref=span, send_sem=psend_sem.at[event], recv_sem=precv_sem.at[event],
             device_id={"att": peer, "emb": me_e}, device_id_type=MESH)
 
-    def u_copy(flat):
+    def u_copy(target):
         return pltpu.make_async_remote_copy(
             src_ref=urecv.at[me], dst_ref=urecv.at[me], send_sem=usend_sem, recv_sem=urecv_sem,
-            device_id=device_of(flat), device_id_type=MESH)
+            device_id=target, device_id_type=MESH)
 
     def send(lo, hi, event):
         def to_emb(j, carry):
             q_copy(lo, hi, event, lax.rem(me_e + j, n_emb)).start()
             return carry
 
-        def to_att(j, carry):
-            p_copy(lo, hi, event, lax.rem(me_a + j, n_att)).start()
-            return carry
-
-        lax.fori_loop(1, n_emb, to_emb, 0)
-        lax.fori_loop(1, n_att, to_att, 0)
+        if hi < n_mats:
+            lax.fori_loop(1, n_emb, to_emb, 0)
+        else:
+            for s in emb_steps:
+                q_copy(lo, hi, event, emb_at[s]).start()
+        for k in range(1, n_att):
+            p_copy(lo, hi, event, att_at[k]).start()
 
     def wait_bytes(ref, sem):
         pltpu.make_async_copy(ref, ref, sem).wait()
@@ -200,27 +260,20 @@
         return u_row
 
     groups = [(MATS * layer, MATS * (layer + 1)) for layer in range(layers - 1)]
-    groups += [(n_mats - MATS, n_mats - 1), (n_mats - 1, n_mats)]
+    groups += [(n_mats - MATS, n_mats - 2), (n_mats - 2, n_mats - 1), (n_mats - 1, n_mats)]
     u_row = jnp.zeros((1, LANES), jnp.float32)
     for event, (lo, hi) in enumerate(groups):
         lax.fori_loop(lo, hi, stream, 0)
-        if event == 0:
-            pl.semaphore_wait(barrier, n_dev - 1)
         send(lo, hi, event)
-        if event == 0:
-            for copy in small + w_copies:
-                copy.wait()
-        else:
-            u_row = process(*groups[event - 1], event - 1, u_row)
-    u_row = process(*groups[-1], len(groups) - 1, u_row)
+    for copy in small + w_copies:
+        copy.wait()
+    for event, (lo, hi) in enumerate(groups):
+        u_row = process(lo, hi, event, u_row)
 
     urecv[me] = u_row
 
-    def to_all(j, carry):
-        u_copy(lax.rem(me + j, n_dev)).start()
-        return carry
-
-    lax.fori_loop(1, n_dev, to_all, 0)
+    for k, s in all_steps:
+        u_copy({"att": att_at[k], "emb": emb_at[s]}).start()
     wait_bytes(urecv.at[pl.ds(0, n_dev - 1)], urecv_sem)
     total = urecv[0]
     for peer in range(1, n_dev):
@@ -232,18 +285,34 @@
     rms_u = jnp.sqrt(mean_row * total / n_elems)
     rms_w = jnp.sqrt(w_total / n_elems)
     scale = rel_step * jnp.maximum(EPS_SCALE, rms_w) / jnp.maximum(1.0, rms_u / clip_limit) * jnp.sqrt(mean_row)
-    for mat in range(n_mats):
-        layer, kind = mat // MATS, mat % MATS
-        factor = scale[:, mat:mat + 1]
-        if kind == MATS - 1:
-            wo_new[layer] = wov[layer] - factor * g[mat]
-        else:
-            wq_new[layer, kind] = wqv[layer, kind] - factor * g[mat]
-
+    scale_row[...] = scale
+
+    for mat in range(n_mats - RING, n_mats):
+        pass_copy(mat % RING).wait_send()
     for event, (lo, hi) in enumerate(groups):
         wait_bytes(qrecv.at[pl.ds(0, n_emb - 1), pl.ds(lo, hi - lo)], qsend_sem.at[event])
         wait_bytes(precv.at[pl.ds(0, n_att - 1), pl.ds(lo, hi - lo)], psend_sem.at[event])
     wait_bytes(urecv.at[pl.ds(0, n_dev - 1)], usend_sem)
+
+
+def update_kernel(wqv, wov, g, scale_row, *refs):
+    stats, wq_new, wo_new, stats_new, wq_out, wo_out, sems = refs[:4], refs[4], refs[5], refs[6:10], *refs[10:]
+    copies = [pltpu.make_async_copy(src, dst, sems.at[k]) for k, (src, dst) in enumerate(zip(stats, stats_new))]
+    for copy in copies:
+        copy.start()
+    for mat in range(g.shape[0]):
+        layer, kind = mat // MATS, mat % MATS
+        step = scale_row[:, mat:mat + 1] * g[mat]
+        if kind == MATS - 1:
+            wo_out[layer] = wov[layer] - step
+            copy = pltpu.make_async_copy(wo_out.at[layer], wo_new.at[layer], sems.at[len(stats) + mat])
+        else:
+            wq_out[layer, kind] = wqv[layer, kind] - step
+            copy = pltpu.make_async_copy(wq_out.at[layer, kind], wq_new.at[layer, kind], sems.at[len(stats) + mat])
+        copy.start()
+        copies.append(copy)
+    for copy in copies:
+        copy.wait()
 
 
 def solution(mesh):
@@ -275,31 +344,31 @@
         f32, bf16 = jnp.float32, jnp.bfloat16
         layers, tokens, p_loc = x_in.shape
         q_loc = x_attn.shape[2]
-        n_mats, n_groups = layers * MATS, layers + 1
+        n_mats, n_groups = layers * MATS, layers + 2
+        rows = tokens // PIECES
         args = (
             jnp.swapaxes(x_in, 1, 2), jnp.swapaxes(dy_out, 1, 2), dy_qkv, x_attn,
             w_qkv, jnp.swapaxes(w_out, 1, 2),
             jnp.swapaxes(r_qkv, 0, 1), jnp.swapaxes(c_qkv, 0, 1), r_out, c_out, hyper_params.reshape(1, 3),
         )
+        args = tuple(pltpu.with_memory_space_constraint(a, pltpu.HBM) for a in args)
         sds = jax.ShapeDtypeStruct
         wo_shape = (layers, p_loc, q_loc)
         rq_shape, cq_shape = (3, layers, p_loc), (3, layers, q_loc)
-        out_shape = (
-            sds(w_qkv.shape, f32), sds(wo_shape, f32), sds(rq_shape, f32), sds(cq_shape, f32),
-            sds(r_out.shape, f32), sds(c_out.shape, f32),
-        )
+        w_shape = (sds(w_qkv.shape, f32), sds(wo_shape, f32))
+        stat_shape = (sds(rq_shape, f32), sds(cq_shape, f32), sds(r_out.shape, f32), sds(c_out.shape, f32))
+        held = (*w_shape, sds((n_mats, p_loc, q_loc), f32), sds((1, LANES), f32), *stat_shape)
         dma = pltpu.SemaphoreType.DMA
         outs = pl.pallas_call(
             functools.partial(adafactor_kernel, n_att, n_emb),
-            out_shape=out_shape,
+            out_shape=held,
             in_specs=[pl.BlockSpec(memory_space=pltpu.HBM)] * len(args),
-            out_specs=[pl.BlockSpec(memory_space=pltpu.VMEM)] * len(out_shape),
+            out_specs=[pl.BlockSpec(memory_space=pltpu.VMEM)] * len(held),
             scratch_shapes=[
-                pltpu.VMEM((SLOTS, tokens, q_loc), bf16),
+                pltpu.VMEM((SLOTS, tokens - 2 * rows, q_loc), bf16),
+                pltpu.VMEM((RING, rows, q_loc), bf16),
+                pltpu.VMEM((RING, rows, q_loc), bf16),
                 pltpu.VMEM((2 * layers, p_loc, tokens), bf16),
-                pltpu.VMEM((n_mats, p_loc, q_loc), f32),
-                pltpu.VMEM(w_qkv.shape, f32),
-                pltpu.VMEM(wo_shape, f32),
                 pltpu.VMEM(rq_shape, f32),
                 pltpu.VMEM(cq_shape, f32),
                 pltpu.VMEM(r_out.shape, f32),
@@ -308,13 +377,25 @@
                 pltpu.VMEM((n_emb, n_mats, q_loc // LANES, LANES), f32),
                 pltpu.VMEM((n_att, n_mats, 1, LANES), f32),
                 pltpu.VMEM((n_att * n_emb, 1, LANES), f32),
-                dma((SLOTS, PIECES)), dma((2 * layers,)), dma((2,)), dma((5,)),
+                dma((SLOTS, PIECES - 2)), dma((RING,)), dma((RING,)), dma((RING,)), pltpu.SemaphoreType.REGULAR,
+                dma((2 * layers,)), dma((2,)), dma((5,)),
                 dma((n_groups,)), dma((n_groups,)), dma((n_groups,)), dma((n_groups,)), dma(()), dma(()),
             ],
             compiler_params=pltpu.CompilerParams(
-                collective_id=0, has_side_effects=True, vmem_limit_bytes=48 * 1024 * 1024),
+                collective_id=0, has_side_effects=True, vmem_limit_bytes=42 * 1024 * 1024),
             name="adafactor",
         )(*args)
+        outs = pl.pallas_call(
+            update_kernel,
+            out_shape=(*w_shape, *stat_shape),
+            in_specs=[pl.BlockSpec(memory_space=pltpu.VMEM)] * len(held),
+            out_specs=[pl.BlockSpec(memory_space=pltpu.HBM)] * (len(w_shape) + len(stat_shape)),
+            scratch_shapes=[
+                pltpu.VMEM(w_qkv.shape, f32), pltpu.VMEM(wo_shape, f32), dma((len(stat_shape) + n_mats,)),
+            ],
+            compiler_params=pltpu.CompilerParams(vmem_limit_bytes=4 * 1024 * 1024),
+            name="update",
+        )(*outs)
         return (
             outs[0], jnp.swapaxes(outs[1], 1, 2), jnp.swapaxes(outs[2], 0, 1), jnp.swapaxes(outs[3], 0, 1),
             outs[4], outs[5],

time: 67 us -> 52.6 us (0.79)
  local copies, waits for them, and re-layouts: 10.6 us -> 0 us
  Pallas kernels: 55.4 us -> 51.8 us
    unnamed x20 -> x0, local copies, waits for them, and re-layouts: 10.6 us -> none
    pallas_call x1, Pallas kernels: 55.4 us -> 50.1 us  [local_run(): pl.pallas_call(functools.partial(adafactor_kernel, n_att, n_emb), out_sha...]
    pallas_call x0 -> x1, Pallas kernels: none -> 1.76 us  [local_run(): pl.pallas_call(update_kernel, out_shape=(*w_shape, *stat_shape), in_specs...]
where the time goes in v2:
time: 52.6 us; the launch traced here: 52.5 us
  Pallas kernels  51.8 us (98%)
  between operations  0.64 us (1%)
    pallas_call x1, Pallas kernels, local_run(): pl.pallas_call(functools.partial(adafactor_kernel, n_att, n_emb), out_sha...  50.1 us
    pallas_call x1, Pallas kernels, local_run(): pl.pallas_call(update_kernel, out_shape=(*w_shape, *stat_shape), in_specs...  1.76 us

profile of v2, /device:TPU:1, one launch (start us, length us, event | category | flops | bytes accessed | tf_op | source)
XLA Modules:
  0.0 52.5 jit_solution(7217163320190633442)
XLA Ops:
  0.6 50.1 %adafactor.1 = (f32[4,3,80,512]{3,2,1,0:T(8,128)S(1)}, f32[4,80,512]{2,1,0:T(8,128)S(1)}, f32[16,80,512]{2,1,0:T(8,128)S(1)}, f32[1,128]{1,0:T(1,128)S(1)}, f32[...) custom-call(bf16[4,80,6144]{2,1,0:T(8,128)(2,1)} %bitcast.9, ...), custom_call_target="tpu_custom_call" | custom-call | tf_op jit(solution)/shard_map/adafactor/pallas_call | solution.py:362
  50.7 1.8 %update.1 = (f32[4,3,80,512]{3,2,1,0:T(8,128)}, f32[4,80,512]{2,1,0:T(8,128)}, f32[3,4,80]{2,1,0:T(4,128)}, f32[3,4,512]{2,1,0:T(4,128)}, f32[4,512]{1,0:T(4,128)}, /*index=5*/f32[4,80]{1,0:T(4,128)}) custom-call(f32[4,3,80,512]{3,2,1,0:T(8,128)S(1)} %get-tuple-element.20.wqv, f32[4,80,512]{2,1,0:T(8,128)S(1)} %get-tuple-element.21.wov, ...), custom_call_target="tpu_custom_call" | custom-call | tf_op jit(solution)/shard_map/update/pallas_call | solution.py:388

commit v3 on v2

--- a/solution.py
+++ b/solution.py
@@ -10,17 +10,18 @@
 EPS_SCALE = 1e-3
 LANES = 128
 MATS = 4
-SLOTS = 4
+SLOTS = 3
 PIECES = 6
-RING = 6
-LEAD = 3
+RING = 5
+LEAD = 1
+EARLY = 2
 MESH = pl.DeviceIdType.MESH
 
 
 def adafactor_kernel(
     n_att, n_emb,
     xt, dt, dyq, xa, wq, wo, rq, cq, ro, co, hyp,
-    wqv, wov, g, scale_row, rq_new, cq_new, ro_new, co_new,
+    wqv, wov, g, scale_rows, rq_new, cq_new, ro_new, co_new,
     bbuf, fbuf, rbuf, abuf, rqv, cqv, rov, cov, hv, qrecv, precv, urecv,
     bsem, fsem, fsend_sem, rsem, free_sem, asem, wsem, ssem,
     qsend_sem, qrecv_sem, psend_sem, precv_sem, usend_sem, urecv_sem,
@@ -45,39 +46,37 @@
     def start_pass(src, slot):
         pltpu.make_async_copy(src.at[own_part], fbuf.at[slot], fsem.at[slot]).start()
 
-    def start_main(src, slot):
-        for k in range(main):
-            part = pl.ds(k * rows, rows)
-            pltpu.make_async_copy(src.at[part], bbuf.at[slot, part], bsem.at[slot, k]).start()
-
-    def of_mat(start, mat, slot):
+    def start_got(src, slot):
+        pltpu.make_async_copy(src.at[got_part], rbuf.at[slot], rsem.at[slot]).start()
+
+    def start_piece(src, slot, k):
+        part = pl.ds(k * rows, rows)
+        pltpu.make_async_copy(src.at[part], bbuf.at[slot, part], bsem.at[slot, k]).start()
+
+    def of_mat(start, mat, slot, *more):
         layer, kind = mat // MATS, lax.rem(mat, MATS)
 
         @pl.when(kind < MATS - 1)
         def _():
-            start(dyq.at[layer, kind], slot)
+            start(dyq.at[layer, kind], slot, *more)
 
         @pl.when(kind == MATS - 1)
         def _():
-            start(xa.at[layer], slot)
+            start(xa.at[layer], slot, *more)
 
     def source(mat):
         return xa.at[mat // MATS] if mat % MATS == MATS - 1 else dyq.at[mat // MATS, mat % MATS]
 
     start_a(xt, 0, 0)
-    for mat in range(SLOTS):
-        start_pass(source(mat), mat)
-        start_main(source(mat), mat)
-    start_a(dt, 0, 1)
-    for mat in range(SLOTS, RING):
-        start_pass(source(mat), mat)
+    for k in range(main):
+        start_piece(source(0), 0, k)
+    start_pass(source(0), 0)
+    start_got(source(0), 0)
     small = [
         pltpu.make_async_copy(src, dst, ssem.at[k])
         for k, (src, dst) in enumerate([(rq, rqv), (cq, cqv), (ro, rov), (co, cov), (hyp, hv)])
     ]
     w_copies = [pltpu.make_async_copy(wq, wqv, wsem.at[0]), pltpu.make_async_copy(wo, wov, wsem.at[1])]
-    for copy in small + w_copies:
-        copy.start()
 
     side = 4
     att_at = [lax.rem(me_a + k, n_att) for k in range(n_att)]
@@ -101,66 +100,56 @@
     for k, s in all_steps:
         pl.semaphore_signal(
             barrier, inc=1, device_id={"att": att_at[k], "emb": emb_at[s]}, device_id_type=MESH)
-    pl.semaphore_wait(barrier, n_dev - 1)
+    for k in range(main):
+        start_piece(source(1), 1, k)
+    start_pass(source(1), 1)
+    start_got(source(1), 1)
+    start_pass(source(EARLY), EARLY)
 
     def pass_copy(slot):
         return pltpu.make_async_remote_copy(
             src_ref=fbuf.at[slot], dst_ref=rbuf.at[slot], send_sem=fsend_sem.at[slot], recv_sem=rsem.at[slot],
             device_id=partner, device_id_type=MESH)
 
-    def pass_on(slot):
+    def wait_pass(slot):
         pltpu.make_async_copy(dyq.at[0, 0, pl.ds(0, rows)], fbuf.at[slot], fsem.at[slot]).wait()
-        pass_copy(slot).start()
-
-    for mat in range(LEAD):
-        pass_on(mat)
-
-    def stream(mat, carry):
-        slot, ring = lax.rem(mat, SLOTS), lax.rem(mat, RING)
-        layer, kind = mat // MATS, lax.rem(mat, MATS)
-        a_slot = 2 * layer + kind // (MATS - 1)
-        ahead = mat + LEAD
-
-        @pl.when(ahead < n_mats)
-        def _():
-            @pl.when(ahead >= RING)
-            def _():
-                pl.semaphore_wait(free_sem, 1)
-
-            pass_on(lax.rem(ahead, RING))
+
+    def a_slot(mat):
+        return 2 * lax.rem(mat // MATS, 2) + lax.rem(mat, MATS) // (MATS - 1)
+
+    def product(mat, part, b):
+        return jnp.dot(abuf[a_slot(mat), :, part], b, preferred_element_type=jnp.float32)
+
+    def ready_a(mat):
+        kind, layer = lax.rem(mat, MATS), mat // MATS
 
         @pl.when(lax.rem(kind, MATS - 1) == 0)
         def _():
-            pltpu.make_async_copy(xt.at[0], abuf.at[a_slot], asem.at[a_slot]).wait()
-
-        @pl.when((kind == 0) & (layer < layers - 1))
-        def _():
-            start_a(xt, layer + 1, 2 * layer + 2)
-            start_a(dt, layer + 1, 2 * layer + 3)
-
-        def product(a_part, b):
-            return jnp.dot(abuf[a_slot, :, a_part], b, preferred_element_type=jnp.float32)
-
-        acc = product(own_part, fbuf[ring])
+            pltpu.make_async_copy(xt.at[0], abuf.at[a_slot(mat)], asem.at[a_slot(mat)]).wait()
+
+        @pl.when((kind == 2) & (layer < layers - 1))
+        def _():
+            start_a(xt, layer + 1, 2 * lax.rem(layer + 1, 2))
+            start_a(dt, layer + 1, 2 * lax.rem(layer + 1, 2) + 1)
+
+    def read_part(mat):
+        slot = lax.rem(mat, SLOTS)
+        acc = jnp.zeros((p_loc, q_loc), jnp.float32)
+        later = mat + SLOTS - 1
         for k in range(main):
             part = pl.ds(k * rows, rows)
             pltpu.make_async_copy(dyq.at[0, 0, part], bbuf.at[slot, part], bsem.at[slot, k]).wait()
-            acc += product(part, bbuf[slot, part, :])
-        pass_copy(ring).wait_recv()
-        acc += product(got_part, rbuf[ring])
-        g[mat] = acc
-
-        @pl.when(mat + RING < n_mats)
-        def _():
-            pl.semaphore_signal(free_sem, inc=1, device_id=partner, device_id_type=MESH)
-            pass_copy(ring).wait_send()
-            of_mat(start_pass, mat + RING, ring)
-
-        @pl.when(mat + SLOTS < n_mats)
-        def _():
-            of_mat(start_main, mat + SLOTS, slot)
-
-        q_sq = acc * acc + EPS_SQUARE
+
+            @pl.when(later < n_mats)
+            def _():
+                of_mat(start_piece, later, lax.rem(later, SLOTS), k)
+
+            acc += product(mat, part, bbuf[slot, part, :])
+        return acc
+
+    def statistics(mat):
+        block = g[mat]
+        q_sq = block * block + EPS_SQUARE
         q_part = jnp.sum(q_sq, axis=0, keepdims=True)
         folded = q_sq[:, :LANES]
         for k in range(1, q_rows):
@@ -169,18 +158,76 @@
         for k in range(q_rows):
             qrecv[me_e, mat, k:k + 1, :] = q_part[:, k * LANES:(k + 1) * LANES]
         precv[me_a, mat] = jnp.sum(padded.T, axis=0, keepdims=True)
+
+    def early(mat):
+        ready_a(mat)
+        acc = read_part(mat)
+        wait_pass(mat)
+        acc += product(mat, own_part, fbuf[mat])
+        pltpu.make_async_copy(dyq.at[0, 0, pl.ds(0, rows)], rbuf.at[mat], rsem.at[mat]).wait()
+        g[mat] = acc + product(mat, got_part, rbuf[mat])
+
+    early(0)
+    start_a(dt, 0, 1)
+    start_pass(source(EARLY + 1), EARLY + 1)
+    statistics(0)
+    early(1)
+    for mat in range(EARLY + 2, RING):
+        start_pass(source(mat), mat)
+    pl.semaphore_wait(barrier, n_dev - 1)
+    for mat in range(EARLY, EARLY + LEAD):
+        wait_pass(mat)
+        pass_copy(mat).start()
+    for mat in range(EARLY):
+        pl.semaphore_signal(free_sem, inc=1, device_id=partner, device_id_type=MESH)
+        start_pass(source(mat + RING), mat)
+    for copy in small + w_copies:
+        copy.start()
+
+    def pass_ahead(mat):
+        ahead = mat + LEAD
+
+        @pl.when(ahead < n_mats)
+        def _():
+            @pl.when(ahead >= RING)
+            def _():
+                pl.semaphore_wait(free_sem, 1)
+
+            wait_pass(lax.rem(ahead, RING))
+            pass_copy(lax.rem(ahead, RING)).start()
+
+    def add_passed(mat, acc):
+        ring = lax.rem(mat, RING)
+        pass_copy(ring).wait_recv()
+        g[mat] = acc + product(mat, got_part, rbuf[ring])
+
+        @pl.when(mat + RING < n_mats)
+        def _():
+            pl.semaphore_signal(free_sem, inc=1, device_id=partner, device_id_type=MESH)
+            pass_copy(ring).wait_send()
+            of_mat(start_pass, mat + RING, ring)
+
+    def stream(mat, carry):
+        pass_ahead(mat)
+        ready_a(mat)
+        acc = product(mat, own_part, fbuf[lax.rem(mat, RING)])
+        statistics(mat - 1)
+        add_passed(mat, acc + read_part(mat))
         return carry
+
+    def wave_of(event):
+        return max(event - layers + 2, 0)
 
     def q_copy(lo, hi, event, peer):
         span = qrecv.at[me_e, pl.ds(lo, hi - lo)]
         return pltpu.make_async_remote_copy(
-            src_ref=span, dst_ref=span, send_sem=qsend_sem.at[event], recv_sem=qrecv_sem.at[event],
+            src_ref=span, dst_ref=span, send_sem=qsend_sem, recv_sem=qrecv_sem.at[wave_of(event)],
             device_id={"att": me_a, "emb": peer}, device_id_type=MESH)
 
     def p_copy(lo, hi, event, peer):
         span = precv.at[me_a, pl.ds(lo, hi - lo)]
         return pltpu.make_async_remote_copy(
-            src_ref=span, dst_ref=span, send_sem=psend_sem.at[event], recv_sem=precv_sem.at[event],
+            src_ref=span, dst_ref=span, send_sem=psend_sem, recv_sem=precv_sem.at[wave_of(event)],
             device_id={"att": peer, "emb": me_e}, device_id_type=MESH)
 
     def u_copy(target):
@@ -189,15 +236,8 @@
             device_id=target, device_id_type=MESH)
 
     def send(lo, hi, event):
-        def to_emb(j, carry):
-            q_copy(lo, hi, event, lax.rem(me_e + j, n_emb)).start()
-            return carry
-
-        if hi < n_mats:
-            lax.fori_loop(1, n_emb, to_emb, 0)
-        else:
-            for s in emb_steps:
-                q_copy(lo, hi, event, emb_at[s]).start()
+        for s in emb_steps:
+            q_copy(lo, hi, event, emb_at[s]).start()
         for k in range(1, n_att):
             p_copy(lo, hi, event, att_at[k]).start()
 
@@ -206,9 +246,9 @@
 
     lane = lax.broadcasted_iota(jnp.int32, (1, LANES), 1)
 
-    def process(lo, hi, event, u_row):
-        wait_bytes(qrecv.at[pl.ds(0, n_emb - 1), pl.ds(lo, hi - lo)], qrecv_sem.at[event])
-        wait_bytes(precv.at[pl.ds(0, n_att - 1), pl.ds(lo, hi - lo)], precv_sem.at[event])
+    def process(lo, hi, wave, u_row):
+        wait_bytes(qrecv.at[pl.ds(0, n_emb - 1), pl.ds(lo, hi - lo)], qrecv_sem.at[wave])
+        wait_bytes(precv.at[pl.ds(0, n_att - 1), pl.ds(lo, hi - lo)], precv_sem.at[wave])
         beta = hv[0:1, 0:1]
         for mat in range(lo, hi):
             layer, kind = mat // MATS, mat % MATS
@@ -260,15 +300,22 @@
         return u_row
 
     groups = [(MATS * layer, MATS * (layer + 1)) for layer in range(layers - 1)]
-    groups += [(n_mats - MATS, n_mats - 2), (n_mats - 2, n_mats - 1), (n_mats - 1, n_mats)]
+    groups += [(n_mats - MATS, n_mats - 2), (n_mats - 2, n_mats)]
     u_row = jnp.zeros((1, LANES), jnp.float32)
+    done = EARLY
     for event, (lo, hi) in enumerate(groups):
-        lax.fori_loop(lo, hi, stream, 0)
+        upto = min(hi + 1, n_mats)
+        if hi < n_mats:
+            lax.fori_loop(done, upto, stream, 0)
+        else:
+            stream(n_mats - 1, 0)
+            statistics(n_mats - 1)
+        done = upto
         send(lo, hi, event)
     for copy in small + w_copies:
         copy.wait()
-    for event, (lo, hi) in enumerate(groups):
-        u_row = process(lo, hi, event, u_row)
+    for wave, (lo, hi) in enumerate([(0, n_mats - MATS), *groups[-2:]]):
+        u_row = process(lo, hi, wave, u_row)
 
     urecv[me] = u_row
 
@@ -285,24 +332,23 @@
     rms_u = jnp.sqrt(mean_row * total / n_elems)
     rms_w = jnp.sqrt(w_total / n_elems)
     scale = rel_step * jnp.maximum(EPS_SCALE, rms_w) / jnp.maximum(1.0, rms_u / clip_limit) * jnp.sqrt(mean_row)
-    scale_row[...] = scale
+    scale_rows[...] = jnp.broadcast_to(scale, (LANES, LANES)).T[:n_mats, :]
 
     for mat in range(n_mats - RING, n_mats):
         pass_copy(mat % RING).wait_send()
-    for event, (lo, hi) in enumerate(groups):
-        wait_bytes(qrecv.at[pl.ds(0, n_emb - 1), pl.ds(lo, hi - lo)], qsend_sem.at[event])
-        wait_bytes(precv.at[pl.ds(0, n_att - 1), pl.ds(lo, hi - lo)], psend_sem.at[event])
+    wait_bytes(qrecv.at[pl.ds(0, n_emb - 1)], qsend_sem)
+    wait_bytes(precv.at[pl.ds(0, n_att - 1)], psend_sem)
     wait_bytes(urecv.at[pl.ds(0, n_dev - 1)], usend_sem)
 
 
-def update_kernel(wqv, wov, g, scale_row, *refs):
+def update_kernel(wqv, wov, g, scale_rows, *refs):
     stats, wq_new, wo_new, stats_new, wq_out, wo_out, sems = refs[:4], refs[4], refs[5], refs[6:10], *refs[10:]
     copies = [pltpu.make_async_copy(src, dst, sems.at[k]) for k, (src, dst) in enumerate(zip(stats, stats_new))]
     for copy in copies:
         copy.start()
     for mat in range(g.shape[0]):
         layer, kind = mat // MATS, mat % MATS
-        step = scale_row[:, mat:mat + 1] * g[mat]
+        step = jnp.concatenate([scale_rows[mat:mat + 1, :]] * (g.shape[2] // LANES), axis=1) * g[mat]
         if kind == MATS - 1:
             wo_out[layer] = wov[layer] - step
             copy = pltpu.make_async_copy(wo_out.at[layer], wo_new.at[layer], sems.at[len(stats) + mat])
@@ -344,7 +390,7 @@
         f32, bf16 = jnp.float32, jnp.bfloat16
         layers, tokens, p_loc = x_in.shape
         q_loc = x_attn.shape[2]
-        n_mats, n_groups = layers * MATS, layers + 2
+        n_mats = layers * MATS
         rows = tokens // PIECES
         args = (
             jnp.swapaxes(x_in, 1, 2), jnp.swapaxes(dy_out, 1, 2), dy_qkv, x_attn,
@@ -357,7 +403,7 @@
         rq_shape, cq_shape = (3, layers, p_loc), (3, layers, q_loc)
         w_shape = (sds(w_qkv.shape, f32), sds(wo_shape, f32))
         stat_shape = (sds(rq_shape, f32), sds(cq_shape, f32), sds(r_out.shape, f32), sds(c_out.shape, f32))
-        held = (*w_shape, sds((n_mats, p_loc, q_loc), f32), sds((1, LANES), f32), *stat_shape)
+        held = (*w_shape, sds((n_mats, p_loc, q_loc), f32), sds((n_mats, LANES), f32), *stat_shape)
         dma = pltpu.SemaphoreType.DMA
         outs = pl.pallas_call(
             functools.partial(adafactor_kernel, n_att, n_emb),
@@ -368,7 +414,7 @@
                 pltpu.VMEM((SLOTS, tokens - 2 * rows, q_loc), bf16),
                 pltpu.VMEM((RING, rows, q_loc), bf16),
                 pltpu.VMEM((RING, rows, q_loc), bf16),
-                pltpu.VMEM((2 * layers, p_loc, tokens), bf16),
+                pltpu.VMEM((4, p_loc, tokens), bf16),
                 pltpu.VMEM(rq_shape, f32),
                 pltpu.VMEM(cq_shape, f32),
                 pltpu.VMEM(r_out.shape, f32),
@@ -378,8 +424,8 @@
                 pltpu.VMEM((n_att, n_mats, 1, LANES), f32),
                 pltpu.VMEM((n_att * n_emb, 1, LANES), f32),
                 dma((SLOTS, PIECES - 2)), dma((RING,)), dma((RING,)), dma((RING,)), pltpu.SemaphoreType.REGULAR,
-                dma((2 * layers,)), dma((2,)), dma((5,)),
-                dma((n_groups,)), dma((n_groups,)), dma((n_groups,)), dma((n_groups,)), dma(()), dma(()),
+                dma((4,)), dma((2,)), dma((5,)),
+                dma(()), dma((3,)), dma(()), dma((3,)), dma(()), dma(()),
             ],
             compiler_params=pltpu.CompilerParams(
                 collective_id=0, has_side_effects=True, vmem_limit_bytes=42 * 1024 * 1024),

time: 52.6 us -> 50.2 us (0.954)
  Pallas kernels: 51.8 us -> 49.5 us
    pallas_call x1, Pallas kernels: 50.1 us -> 47.8 us  [local_run(): pl.pallas_call(functools.partial(adafactor_kernel, n_att, n_emb), out_sha...]
where the time goes in v3:
time: 50.2 us; the launch traced here: 50.1 us
  Pallas kernels  49.5 us (99%)
  between operations  0.64 us (1%)
    pallas_call x1, Pallas kernels, local_run(): pl.pallas_call(functools.partial(adafactor_kernel, n_att, n_emb), out_sha...  47.8 us
    pallas_call x1, Pallas kernels, local_run(): pl.pallas_call(update_kernel, out_shape=(*w_shape, *stat_shape), in_specs...  1.67 us

profile of v3, /device:TPU:1, one launch (start us, length us, event | category | flops | bytes accessed | tf_op | source)
XLA Modules:
  0.0 50.1 jit_solution(15088704352439255575)
XLA Ops:
  0.6 47.8 %adafactor.1 = (f32[4,3,80,512]{3,2,1,0:T(8,128)S(1)}, f32[4,80,512]{2,1,0:T(8,128)S(1)}, f32[16,80,512]{2,1,0:T(8,128)S(1)}, f32[16,128]{1,0:T(8,128)S(1)}, f32...) custom-call(bf16[4,80,6144]{2,1,0:T(8,128)(2,1)} %bitcast.9, ...), custom_call_target="tpu_custom_call" | custom-call | tf_op jit(solution)/shard_map/adafactor/pallas_call | solution.py:408
  48.5 1.7 %update.1 = (f32[4,3,80,512]{3,2,1,0:T(8,128)}, f32[4,80,512]{2,1,0:T(8,128)}, f32[3,4,80]{2,1,0:T(4,128)}, f32[3,4,512]{2,1,0:T(4,128)}, f32[4,512]{1,0:T(4,128)}, /*index=5*/f32[4,80]{1,0:T(4,128)}) custom-call(f32[4,3,80,512]{3,2,1,0:T(8,128)S(1)} %get-tuple-element.20.wqv, f32[4,80,512]{2,1,0:T(8,128)S(1)} %get-tuple-element.21.wov, ...), custom_call_target="tpu_custom_call" | custom-call | tf_op jit(solution)/shard_map/update/pallas_call | solution.py:434

commit v4 on v3

--- a/solution.py
+++ b/solution.py
@@ -16,6 +16,12 @@
 LEAD = 1
 EARLY = 2
 MESH = pl.DeviceIdType.MESH
+
+
+def tree_sum(terms):
+    while len(terms) > 1:
+        terms = [a + b for a, b in zip(terms[::2], terms[1::2])] + terms[len(terms) // 2 * 2:]
+    return terms[0]
 
 
 def adafactor_kernel(
@@ -181,7 +187,7 @@
     for mat in range(EARLY):
         pl.semaphore_signal(free_sem, inc=1, device_id=partner, device_id_type=MESH)
         start_pass(source(mat + RING), mat)
-    for copy in small + w_copies:
+    for copy in small:
         copy.start()
 
     def pass_ahead(mat):
@@ -253,12 +259,8 @@
         for mat in range(lo, hi):
             layer, kind = mat // MATS, mat % MATS
             is_out = kind == MATS - 1
-            q_sum = qrecv[0, mat]
-            for peer in range(1, n_emb):
-                q_sum += qrecv[peer, mat]
-            p_sum = precv[0, mat]
-            for peer in range(1, n_att):
-                p_sum += precv[peer, mat]
+            q_sum = tree_sum([qrecv[peer, mat] for peer in range(n_emb)])
+            p_sum = tree_sum([precv[peer, mat] for peer in range(n_att)])
             q_add = (1.0 - beta) * (q_sum / d_model)
             p_new_all = (1.0 - beta) * (p_sum / inner)
             p_old = cov[layer:layer + 1, :] if is_out else rqv[kind, layer:layer + 1, :]
@@ -309,6 +311,8 @@
             lax.fori_loop(done, upto, stream, 0)
         else:
             stream(n_mats - 1, 0)
+            for copy in w_copies:
+                copy.start()
             statistics(n_mats - 1)
         done = upto
         send(lo, hi, event)
@@ -322,9 +326,7 @@
     for k, s in all_steps:
         u_copy({"att": att_at[k], "emb": emb_at[s]}).start()
     wait_bytes(urecv.at[pl.ds(0, n_dev - 1)], urecv_sem)
-    total = urecv[0]
-    for peer in range(1, n_dev):
-        total += urecv[peer]
+    total = tree_sum([urecv[peer] for peer in range(n_dev)])
     w_total = pltpu.roll(total, LANES - n_mats, 1)
     mean_row = pltpu.roll(total, LANES - 2 * n_mats, 1)
     n_elems = d_model * inner

time: 50.2 us -> 49.4 us (0.984)
  Pallas kernels: 49.5 us -> 48.6 us
    pallas_call x1, Pallas kernels: 47.8 us -> 46.9 us  [local_run(): pl.pallas_call(functools.partial(adafactor_kernel, n_att, n_emb), out_sha...]
where the time goes in v4:
time: 49.4 us; the launch traced here: 49.3 us
  Pallas kernels  48.6 us (98%)
  between operations  0.64 us (1%)
    pallas_call x1, Pallas kernels, local_run(): pl.pallas_call(functools.partial(adafactor_kernel, n_att, n_emb), out_sha...  46.9 us
    pallas_call x1, Pallas kernels, local_run(): pl.pallas_call(update_kernel, out_shape=(*w_shape, *stat_shape), in_specs...  1.67 us

profile of v4, /device:TPU:1, one launch (start us, length us, event | category | flops | bytes accessed | tf_op | source)
XLA Modules:
  0.0 49.3 jit_solution(2998891017652381779)
XLA Ops:
  0.6 46.9 %adafactor.1 = (f32[4,3,80,512]{3,2,1,0:T(8,128)S(1)}, f32[4,80,512]{2,1,0:T(8,128)S(1)}, f32[16,80,512]{2,1,0:T(8,128)S(1)}, f32[16,128]{1,0:T(8,128)S(1)}, f32...) custom-call(bf16[4,80,6144]{2,1,0:T(8,128)(2,1)} %bitcast.9, ...), custom_call_target="tpu_custom_call" | custom-call | tf_op jit(solution)/shard_map/adafactor/pallas_call | solution.py:410
  47.6 1.7 %update.1 = (f32[4,3,80,512]{3,2,1,0:T(8,128)}, f32[4,80,512]{2,1,0:T(8,128)}, f32[3,4,80]{2,1,0:T(4,128)}, f32[3,4,512]{2,1,0:T(4,128)}, f32[4,512]{1,0:T(4,128)}, /*index=5*/f32[4,80]{1,0:T(4,128)}) custom-call(f32[4,3,80,512]{3,2,1,0:T(8,128)S(1)} %get-tuple-element.20.wqv, f32[4,80,512]{2,1,0:T(8,128)S(1)} %get-tuple-element.21.wov, ...), custom_call_target="tpu_custom_call" | custom-call | tf_op jit(solution)/shard_map/update/pallas_call | solution.py:436
